TPU v7x, 32 devices: a whole 2x2x4 slice. The times are simulated.
32 devices in a mesh: rep: 2 (over y), seq: 8 (over z, x), head: 2 (over core).
Axes of the slice: x: 2, y: 2, z: 4, core: 2. Of those that a mesh axis runs over, the one named last changes fastest.
Arguments:
- prompt_query: bfloat16 [2048, 1792], P(('rep', 'seq', 'head')), parts along dimension 0, may hold values from -12 to 12
- prompt_key: bfloat16 [2048, 256], P(('rep', 'seq', 'head')), parts along dimension 0, may hold values from -12 to 12
- prompt_value: bfloat16 [2048, 256], P(('rep', 'seq', 'head')), parts along dimension 0, may hold values from -24 to 24
- prompt_length: int32 [2], P('rep'), parts along dimension 0, may hold values from 512 to 1024
- span_order: int32 [32], P('rep'), parts along dimension 0, may hold values from 0 to 15, each once
- new_query: bfloat16 [32, 1792], P('rep', 'head'), parts along dimension 0, may hold values from -12 to 12
- new_key: bfloat16 [32, 256], P('rep', 'head'), parts along dimension 0, may hold values from -12 to 12
- new_value: bfloat16 [32, 256], P('rep', 'head'), parts along dimension 0, may hold values from -24 to 24
- cache_key: bfloat16 [32, 2, 2048, 128], P('rep', 'head', 'seq'), parts along dimension 0, may hold values from -12 to 12
- cache_value: bfloat16 [32, 2, 2048, 128], P('rep', 'head', 'seq'), parts along dimension 0, may hold values from -24 to 24
- cache_length: int32 [32], P('rep'), parts along dimension 0, may hold values from 1280 to 2048
Outputs:
- prompt_attended: bfloat16 [2048, 1792], P(('rep', 'seq', 'head')), parts along dimension 0
- decode_attended: bfloat16 [32, 1792], P('rep', 'head'), parts along dimension 0
There are 2 independent parts, one for each index of `rep`. A program takes and returns all parts, laid end to end along the dimension named above; each array names one. Nothing has to cross between parts.
Inputs may be any that keep to these rules, and one draw needn't show every extreme that they name: `span_order`: each of the 16 spans stands once.
All inputs are finite; a program needn't handle non-finite values.
Results may differ from a plain program's by a relative error of at most 0.0045.
Values may be sent and summed in bfloat16 or wider, within the bound.
A program may use at most 128 MiB of HBM per device.

v0:
```python
import math

import jax
import jax.numpy as jnp
from jax import lax
from jax.sharding import PartitionSpec as P

HD = 128
QH = 14
KVH = 2


def lookup(span_table, row_ids, span_rows):
    chosen = (
        row_ids[:, None] // span_rows == jnp.arange(span_table.shape[0], dtype=jnp.int32)[None, :]
    )
    picked = jnp.sum(jnp.where(chosen, span_table[None, :], 0), axis=1)
    return picked * span_rows + row_ids % span_rows


def block_size(key_count, span_rows):
    units = key_count // span_rows
    most = max(1, 512 // span_rows)
    best = 1
    for count in range(1, min(units, most) + 1):
        if units % count == 0:
            best = count
    return best * span_rows


def start_state(query_rows, kv_heads, head_group):
    row_max = jnp.full((kv_heads, head_group, query_rows), -1e30, jnp.float32)
    row_total = jnp.zeros((kv_heads, head_group, query_rows), jnp.float32)
    weighted = jnp.zeros((kv_heads, head_group, query_rows, HD), jnp.float32)
    return (row_max, row_total, weighted)


def attend_rows(running, shard_piece, queries, query_pos, span_table, span_rows, length_limit):
    keys_piece, values_piece = shard_piece
    key_count = keys_piece.shape[0]
    kv_heads = queries.shape[1]
    block_rows = block_size(key_count, span_rows)
    score_scale = 1.0 / math.sqrt(HD)

    def advance(carried, block_index):
        first_row = block_index * block_rows
        key_block = lax.dynamic_slice_in_dim(keys_piece, first_row, block_rows, 0).reshape(
            block_rows, kv_heads, HD
        )
        value_block = lax.dynamic_slice_in_dim(values_piece, first_row, block_rows, 0).reshape(
            block_rows, kv_heads, HD
        )
        key_pos = lookup(span_table, first_row + jnp.arange(block_rows, dtype=jnp.int32), span_rows)
        allowed = (key_pos[None, :] <= query_pos[:, None]) & (key_pos[None, :] < length_limit)

        def compute(state_in):
            row_max, row_total, weighted = state_in
            scores = (
                jnp.einsum("rkgd,nkd->kgrn", queries, key_block, preferred_element_type=jnp.float32)
                * score_scale
            )
            scores = jnp.where(allowed, scores, -1e30)
            new_max = jnp.maximum(row_max, jnp.max(scores, axis=-1))
            weights = jnp.where(allowed, jnp.exp(scores - new_max[..., None]), 0.0)
            factor = jnp.exp(row_max - new_max)
            row_total = row_total * factor + jnp.sum(weights, axis=-1)
            weighted = weighted * factor[..., None] + jnp.einsum(
                "kgrn,nkd->kgrd",
                weights.astype(jnp.bfloat16),
                value_block,
                preferred_element_type=jnp.float32,
            )
            return (new_max, row_total, weighted)

        return (lax.cond(jnp.any(allowed), compute, lambda state_in: state_in, carried), None)

    running, _ = lax.scan(advance, running, jnp.arange(key_count // block_rows, dtype=jnp.int32))
    return running


def finish(running, query_pos, length_limit):
    row_max, row_total, weighted = running
    result = weighted / row_total[..., None]
    result = jnp.transpose(result, (2, 0, 1, 3))
    result = jnp.where((query_pos < length_limit)[:, None, None, None], result, 0.0)
    return result.reshape(result.shape[0], -1).astype(jnp.bfloat16)


def per_device(
    prompt_query,
    prompt_key,
    prompt_value,
    prompt_length,
    span_order,
    new_query,
    new_key,
    new_value,
    cache_key,
    cache_value,
    cache_length,
):
    head_group = QH // KVH
    score_scale = 1.0 / math.sqrt(HD)
    length_limit = prompt_length[0]
    span_rows = prompt_query.shape[0]
    kv_heads = prompt_key.shape[1] // HD
    first_row = (lax.axis_index("seq") * lax.axis_size("head") + lax.axis_index("head")) * span_rows
    query_pos = lookup(span_order, first_row + jnp.arange(span_rows, dtype=jnp.int32), span_rows)
    queries = prompt_query.reshape(span_rows, kv_heads, head_group, HD)
    running = attend_rows(
        start_state(span_rows, kv_heads, head_group),
        (
            lax.all_gather(prompt_key, ("seq", "head"), axis=0, tiled=True),
            lax.all_gather(prompt_value, ("seq", "head"), axis=0, tiled=True),
        ),
        queries,
        query_pos,
        span_order,
        span_rows,
        length_limit,
    )
    prompt_attended = finish(running, query_pos, length_limit)
    sessions = new_query.shape[0]
    local_heads = cache_key.shape[1]
    local_ctx = cache_key.shape[2]
    dec_queries = new_query.reshape(sessions, local_heads, head_group, HD)
    cache_pos = lax.axis_index("seq") * local_ctx + jnp.arange(local_ctx, dtype=jnp.int32)
    valid = (cache_pos[None, :] < cache_length[:, None])[:, None, None, :]
    scores = (
        jnp.einsum("skgd,sktd->skgt", dec_queries, cache_key, preferred_element_type=jnp.float32)
        * score_scale
    )
    scores = jnp.where(valid, scores, -1e30)
    row_max = jnp.max(scores, axis=-1)
    weights = jnp.where(valid, jnp.exp(scores - row_max[..., None]), 0.0)
    row_total = jnp.sum(weights, axis=-1)
    weighted = jnp.einsum(
        "skgt,sktd->skgd",
        weights.astype(jnp.bfloat16),
        cache_value,
        preferred_element_type=jnp.float32,
    )
    global_max = lax.pmax(row_max, "seq")
    factor = jnp.exp(row_max - global_max)
    row_total, weighted = lax.psum((row_total * factor, weighted * factor[..., None]), "seq")
    row_max = global_max
    own_score = (
        jnp.einsum(
            "skgd,skd->skg",
            dec_queries,
            new_key.reshape(sessions, local_heads, HD),
            preferred_element_type=jnp.float32,
        )
        * score_scale
    )
    final_max = jnp.maximum(row_max, own_score)
    old_factor = jnp.exp(row_max - final_max)
    own_weight = jnp.exp(own_score - final_max)
    row_total = row_total * old_factor + own_weight
    own_rounded = lax.optimization_barrier(own_weight.astype(jnp.bfloat16)).astype(jnp.float32)
    fresh_value = new_value.reshape(sessions, local_heads, 1, HD).astype(jnp.float32)
    weighted = weighted * old_factor[..., None] + own_rounded[..., None] * fresh_value
    decode_attended = (weighted / row_total[..., None]).reshape(sessions, -1).astype(jnp.bfloat16)
    return (prompt_attended, decode_attended)


def solution(mesh):
    return jax.shard_map(
        per_device,
        mesh=mesh,
        in_specs=(
            P(("rep", "seq", "head"), None),
            P(("rep", "seq", "head"), None),
            P(("rep", "seq", "head"), None),
            P("rep"),
            P("rep"),
            P("rep", "head"),
            P("rep", "head"),
            P("rep", "head"),
            P("rep", "head", "seq", None),
            P("rep", "head", "seq", None),
            P("rep"),
        ),
        out_specs=(P(("rep", "seq", "head"), None), P("rep", "head")),
        check_vma=False,
    )
```

profile of v0, /device:TPU:0, one launch (start us, length us, event | category | flops | bytes accessed | tf_op | source)
XLA Modules:
  0.0 115.9 jit_solution(7205853363123510908)
XLA Ops:
  0.6 0.0 copy-start
  0.6 0.0 copy-start.2
  1.4 0.7 select_reduce_fusion.1
  2.2 24.8 %all_gather.6 = bf16[1024,256]{1,0:T(8,128)(2,1)S(1)} all-gather(bf16[64,256]{1,0:T(8,128)(2,1)} %param.16), channel_id=1, replica_groups=mesh['rep'=2,'seq'=8,'head'=2] {'seq','head'}, dimensions={0}, use_global_device_ids=true | all-gather | bytes 557056 | tf_op jit(solution)/shard_map/all_gather | solution.py:113
  27.0 0.0 copy-start.4
  27.0 0.2 copy.44
  27.2 1.2 %reshape.237 = bf16[64,2,7,128]{3,2,1,0:T(8,128)(2,1)S(1)} reshape(bf16[64,1792]{1,0:T(8,128)(2,1)} %param.15) | data formatting | bytes 458752 | tf_op jit(solution)/shard_map/reshape | solution.py:109
  28.4 0.1 copy.45
  28.5 0.0 copy-done.2
  28.5 18.9 %all_gather.7 = bf16[1024,256]{1,0:T(8,128)(2,1)S(1)} all-gather(bf16[64,256]{1,0:T(8,128)(2,1)S(1)} %copy-done.2), channel_id=1, replica_groups=mesh['rep'=2,'seq'=8,'head'=2] {'seq','head'}, dimensions={0}, use_global_device_ids=true | all-gather | bytes 557056 | tf_op jit(solution)/shard_map/all_gather | solution.py:114
  47.4 0.2 copy.46
  47.7 0.0 copy-done.4
  47.7 0.0 copy-start.3
  47.7 0.0 copy-start.6
  47.7 9.3 %while.16 = (s32[]{:T(128)}, f32[2,7,64]{2,1,0:T(8,128)S(1)}, f32[2,7,64]{2,1,0:T(8,128)S(1)}, f32[2,7,64,128]{3,2,1,0:T(8,128)S(1)}, s32[2]{0:T(128)S(1)}, /*in...) while((s32[]{:T(128)}, f32[2,7,64]{2,1,0:T(8,128)S(1)}, ...), condition=%wide.region_8.9_spmd, body=%wide.region_1.8_spmd.sunk | while | flops 241214208 | bytes 8427149 | solution.py:77
  47.7 0.6 dynamic_slice.30
  49.0 0.1 select_reduce_fusion.3
  49.1 0.7 broadcast_compare_fusion.4
  49.7 0.8 compare_and_fusion.2
  51.2 2.2 %conditional.2 = ((f32[2,7,64]{2,1,0:T(8,128)S(1)}, f32[2,7,64]{2,1,0:T(8,128)S(1)}, f32[2,7,64,128]{3,2,1,0:T(8,128)S(1)})) conditional(s32[]{:T(128)} %convert_element_type.57, (f32[2,7,64]{2,1,0:T(8,128)S(1)}, f32[2,7,64]{2,1,0:T(8,128)S(1)}, f32[2,7,64,128]{3,2,1,0:T(8,128)S(1)}) %tuple.65, (pred[64,512]{1,0:T(8,128)(4,1)S(1)}, s32[]{:T(128)}, ...), branch_computations={%region_4.4_spmd, %region_5.7_spmd} | conditional | flops 241075968 | bytes 8380486 | solution.py:75
  51.3 0.3 constant_dynamic-slice_fusion
  51.6 0.5 fusion
  52.1 0.6 fusion.2
  52.7 0.7 convolution_add_fusion
  53.5 0.6 dynamic_slice.30
  54.7 0.1 select_reduce_fusion.3
  54.8 0.7 broadcast_compare_fusion.4
  55.5 0.8 compare_and_fusion.2
  57.0 0.0 copy-start.1
  57.0 0.2 fusion.20
  57.2 0.0 copy-start.7
  57.3 0.2 copy.47
  57.4 0.0 copy-start.5
  57.4 1.0 convert_element_type.41
  58.4 0.0 copy-done.3
  58.4 0.1 reshape.238
  58.5 0.0 copy-done.6
  58.5 0.1 broadcast_compare_fusion.1
  58.6 0.0 copy-done
  58.6 0.5 fusion.38
  59.0 0.2 fusion.21
  59.2 0.1 copy.52
  59.3 0.1 copy.48
  59.4 21.0 %pmax.7 = f32[16,1,7]{0,2,1:T(8,128)S(1)} all-reduce(f32[16,1,7]{0,2,1:T(8,128)S(1)} %bitcast.92), channel_id=1, replica_groups=mesh['rep'=2,'seq'=8,'head'=2] {'seq'}, use_global_device_ids=true, to_apply=%region_10.11 | all-reduce | flops 112 | bytes 896 | tf_op jit(solution)/shard_map/pmax | solution.py:143
  80.4 0.1 copy.49
  80.5 0.0 copy-done.1
  80.5 0.3 fusion.17
  80.8 33.8 %all-reduce = (f32[16,1,7,128]{3,2,0,1:T(8,128)S(1)}, f32[16,1,7]{0,2,1:T(8,128)S(1)}) all-reduce(f32[16,1,7,128]{3,2,0,1:T(8,128)S(1)} %fusion.17, f32[16,1,7]{0,2,1:T(8,128)S(1)} %get-tuple-element.328), channel_id=1, replica_groups=mesh['rep'=2,'seq'=8,'head'=2] {'seq'}, use_global_device_ids=true, to_apply=%region_11.12 | all-reduce | flops 14448 | bytes 115584 | tf_op jit(solution)/shard_map/psum | solution.py:145
  114.6 0.0 copy-done.7
  114.6 0.1 fusion.27
  114.7 0.1 copy.57
  114.8 0.1 copy.53
  114.9 0.0 copy-done.5
  115.0 0.1 copy.51
  115.0 0.1 copy.50
  115.1 0.1 divide_convert_fusion
  115.2 0.6 copy.66
  (17 shorter events, 0.2 us)
Async XLA Ops:
  0.6 57.9 %copy-start = (bf16[16,1,256,128]{3,2,1,0:T(8,128)(2,1)S(1)}, bf16[16,1,256,128]{3,2,1,0:T(8,128)(2,1)}, u32[]{:S(2)}) copy-start(bf16[16,1,256,128]{3,2,1,0:T(8,128)(2,1)} %param.23) | copy-start | bytes 3145732
  0.6 27.9 %copy-start.2 = (bf16[64,256]{1,0:T(8,128)(2,1)S(1)}, bf16[64,256]{1,0:T(8,128)(2,1)}, u32[]{:S(2)}) copy-start(bf16[64,256]{1,0:T(8,128)(2,1)} %param.17) | copy-start | bytes 98308
  27.0 20.7 %copy-start.4 = (s32[16]{0:T(128)S(1)}, s32[16]{0:T(128)}, u32[]{:S(2)}) copy-start(s32[16]{0:T(128)} %param.19) | copy-start | bytes 196
  47.7 10.7 %copy-start.3 = (bf16[16,896]{1,0:T(8,128)(2,1)S(1)}, bf16[16,896]{1,0:T(8,128)(2,1)}, u32[]{:S(2)}) copy-start(bf16[16,896]{1,0:T(8,128)(2,1)} %param.20) | copy-start | bytes 86020
  47.7 10.8 %copy-start.6 = (s32[16]{0:T(128)S(1)}, s32[16]{0:T(128)}, u32[]{:S(2)}) copy-start(s32[16]{0:T(128)} %param.25) | copy-start | bytes 196
  57.0 23.4 %copy-start.1 = (bf16[16,1,256,128]{3,2,1,0:T(8,128)(2,1)S(1)}, bf16[16,1,256,128]{3,2,1,0:T(8,128)(2,1)}, u32[]{:S(2)}) copy-start(bf16[16,1,256,128]{3,2,1,0:T(8,128)(2,1)} %param.24) | copy-start | bytes 3145732
  57.2 57.4 %copy-start.7 = (bf16[16,128]{1,0:T(8,128)(2,1)S(1)}, bf16[16,128]{1,0:T(8,128)(2,1)}, u32[]{:S(2)}) copy-start(bf16[16,128]{1,0:T(8,128)(2,1)} %param.21) | copy-start | bytes 12292
  57.4 57.5 %copy-start.5 = (bf16[16,128]{1,0:T(8,128)(2,1)S(1)}, bf16[16,128]{1,0:T(8,128)(2,1)}, u32[]{:S(2)}) copy-start(bf16[16,128]{1,0:T(8,128)(2,1)} %param.22) | copy-start | bytes 12292
where the time goes:
time: 116 us
  blocking collectives  98.5 us (85%)
  local copies, waits for them, and re-layouts  5.63 us (5%)
  other arithmetic  5.16 us (4%)
  loops' own time  2.84 us (2%)
  matrix products  2.11 us (2%)
  between operations  1.6 us (1%)
    psum x1, blocking collectives, per_device(): lax.psum((row_total * factor, weighted * factor[..., None]), 'seq')  33.8 us
    all_gather x1, blocking collectives, per_device(): lax.all_gather(prompt_key, ('seq', 'head'), axis=0, tiled=True)  24.8 us
    pmax x1, blocking collectives, per_device(): global_max = lax.pmax(row_max, 'seq')  21 us
    all_gather x1, blocking collectives, per_device(): lax.all_gather(prompt_value, ('seq', 'head'), axis=0, tiled=True)  18.9 us
    another operation x1, loops' own time, attend_rows(): lax.scan(advance, running, jnp.arange(key_count // block_rows, dtype=jnp....  2.77 us

commit v1 on v0

--- a/solution.py
+++ b/solution.py
@@ -1,8 +1,11 @@
+import functools
 import math
 
 import jax
 import jax.numpy as jnp
 from jax import lax
+from jax.experimental import pallas as pl
+from jax.experimental.pallas import tpu as pltpu
 from jax.sharding import PartitionSpec as P
 
 HD = 128
@@ -86,7 +89,7 @@
     return result.reshape(result.shape[0], -1).astype(jnp.bfloat16)
 
 
-def per_device(
+def composed(
     prompt_query,
     prompt_key,
     prompt_value,
@@ -164,9 +167,337 @@
     return (prompt_attended, decode_attended)
 
 
+MESH = pl.DeviceIdType.MESH
+LOW = -1e30
+FAR = 1 << 30
+
+
+def pick(index, table):
+    out = jnp.int32(table[0])
+    for i in range(1, len(table)):
+        out = jnp.where(index == i, jnp.int32(table[i]), out)
+    return out
+
+
+def fused_kernel(
+    outer, inner, cores,
+    pq_hbm, pk_hbm, pv_hbm, length_ref, order_ref, nq_ref, nk_ref, nv_ref, ck_hbm, cv_hbm, clen_ref,
+    out_ref, dec_ref,
+    pq, kbuf, vbuf, ck, cv, qrows, part_out, part_in, done, flat,
+    in_sem, kv_send, kv_recv, part_send, part_recv, done_send, done_recv,
+):
+    group = QH // KVH
+    span = kbuf.shape[1] // (inner * cores)
+    n_seq = outer * inner
+    seq = lax.axis_index("seq")
+    core = lax.axis_index("head")
+    a = seq // inner
+    b = seq % inner
+    log2_scale = math.log2(math.e) / math.sqrt(HD)
+
+    def rows_of(b_, c_):
+        return pl.ds(pl.multiple_of((b_ * cores + c_) * span, span), span)
+
+    def block_id(a_, b_, c_):
+        return (a_ * inner + b_) * cores + c_
+
+    local = [
+        pltpu.make_async_copy(pk_hbm, kbuf.at[a, rows_of(b, core)], in_sem.at[0]),
+        pltpu.make_async_copy(pv_hbm, vbuf.at[a, rows_of(b, core)], in_sem.at[1]),
+        pltpu.make_async_copy(ck_hbm, ck, in_sem.at[2]),
+        pltpu.make_async_copy(cv_hbm, cv, in_sem.at[3]),
+        pltpu.make_async_copy(pq_hbm, pq, in_sem.at[4]),
+    ]
+    for copy in local:
+        copy.start()
+
+    barrier = pltpu.get_barrier_semaphore()
+    for d in range(1, n_seq):
+        pl.semaphore_signal(
+            barrier, inc=1, device_id={"seq": (seq + d) % n_seq}, device_id_type=MESH
+        )
+    for d in range(1, cores):
+        pl.semaphore_signal(
+            barrier, inc=1, device_id={"head": (core + d) % cores}, device_id_type=MESH
+        )
+    local[0].wait()
+    local[1].wait()
+    pl.semaphore_wait(barrier, n_seq - 1 + cores - 1)
+
+    sends = []
+
+    def send(a_, b_, c_, target):
+        block = block_id(a_, b_, c_)
+        for which, buf in ((0, kbuf), (1, vbuf)):
+            ref = buf.at[a_, rows_of(b_, c_)]
+            copy = pltpu.make_async_remote_copy(
+                src_ref=ref,
+                dst_ref=ref,
+                send_sem=kv_send.at[which, len(sends) // 2],
+                recv_sem=kv_recv.at[which, block],
+                device_id=target,
+                device_id_type=MESH,
+            )
+            copy.start()
+            sends.append(copy)
+
+    def await_block(a_, b_, c_):
+        block = block_id(a_, b_, c_)
+        for which, buf in ((0, kbuf), (1, vbuf)):
+            ref = buf.at[a_, rows_of(b_, c_)]
+            pltpu.make_async_remote_copy(
+                src_ref=ref,
+                dst_ref=ref,
+                send_sem=kv_send.at[which, 0],
+                recv_sem=kv_recv.at[which, block],
+                device_id={"seq": seq},
+                device_id_type=MESH,
+            ).wait_recv()
+
+    def to_inner(a_, b_, c_):
+        for d in range(1, inner):
+            send(a_, b_, c_, {"seq": a * inner + (b + d) % inner})
+
+    def to_core(a_, b_, c_):
+        for d in range(1, cores):
+            send(a_, b_, c_, {"head": (core + d) % cores})
+
+    nearest = [sorted(range(outer), key=lambda p, i=i: (abs(p - i), p)) for i in range(outer)]
+    planes = [pick(a, [nearest[i][k] for i in range(outer)]) for k in range(outer)]
+
+    to_inner(a, b, core)
+    for k in range(1, outer):
+        send(a, b, core, {"seq": planes[k] * inner + b})
+    to_core(a, b, core)
+
+    sessions, ctx = ck.shape[0], ck.shape[2]
+    per = sessions // n_seq
+    for h in range(8):
+        if h < group:
+            qrows[pl.ds(h * sessions, sessions), :] = nq_ref[:, h * HD : (h + 1) * HD].astype(
+                jnp.float32
+            )
+        else:
+            qrows[pl.ds(h * sessions, sessions), :] = jnp.zeros((sessions, HD), jnp.float32)
+    local[2].wait()
+    local[3].wait()
+    cache_pos = seq * ctx + lax.broadcasted_iota(jnp.int32, (8, ctx), 1)
+    first = seq == 0
+    nk = nk_ref[...].astype(jnp.float32)
+    nv = nv_ref[...].astype(jnp.float32)
+    inv = 1.0 / math.sqrt(HD)
+    for s in range(sessions):
+        q32 = qrows[pl.ds(s, 8, stride=sessions), :]
+        sc = lax.dot_general(
+            q32.astype(jnp.bfloat16), ck[s, 0], (((1,), (1,)), ((), ())),
+            preferred_element_type=jnp.float32,
+        ) * inv
+        own = jnp.sum(q32 * nk[s : s + 1, :], axis=1, keepdims=True) * inv
+        own = jnp.where(first, own, LOW)
+        valid = cache_pos < clen_ref[s]
+        sc = jnp.where(valid, sc, LOW)
+        top = jnp.maximum(jnp.max(sc, axis=1, keepdims=True), own)
+        w = jnp.where(valid, jnp.exp(sc - top), 0.0)
+        own_w = jnp.where(first, jnp.exp(own - top), 0.0)
+        tot = jnp.sum(w, axis=1, keepdims=True) + own_w
+        o = jnp.dot(w.astype(jnp.bfloat16), cv[s, 0], preferred_element_type=jnp.float32)
+        o = o + own_w.astype(jnp.bfloat16).astype(jnp.float32) * nv[s : s + 1, :]
+        lane = lax.broadcasted_iota(jnp.int32, (8, HD), 1)
+        dst, row = s // per, (s % per) * 8
+        part_out[dst, 0, pl.ds(row, 8), :] = o
+        part_out[dst, 1, pl.ds(row, 8), :] = jnp.where(lane < HD // 2, top, tot)
+
+    part_copies = []
+    for d in range(1, n_seq):
+        peer = (seq + d) % n_seq
+        copy = pltpu.make_async_remote_copy(
+            src_ref=part_out.at[peer],
+            dst_ref=part_in.at[n_seq - 1 - d],
+            send_sem=part_send.at[d - 1],
+            recv_sem=part_recv.at[n_seq - 1 - d],
+            device_id={"seq": peer},
+            device_id_type=MESH,
+        )
+        copy.start()
+        part_copies.append(copy)
+
+    local[4].wait()
+    me_block = block_id(a, b, core)
+    limit = length_ref[0]
+    rows = group * span
+    row_pos = order_ref[me_block] * span + lax.broadcasted_iota(jnp.int32, (rows, 1), 0) % span
+    keys = kbuf.shape[1]
+    lane = lax.broadcasted_iota(jnp.int32, (1, keys), 1)
+    queries = [
+        jnp.concatenate(
+            [pq[:, (g * group + h) * HD : (g * group + h + 1) * HD] for h in range(group)], axis=0
+        )
+        for g in range(KVH)
+    ]
+    state = [None] * KVH
+
+    def attend(a_):
+        base = jnp.zeros((1, keys), jnp.int32)
+        for j in range(inner * cores):
+            base = jnp.where(lane // span == j, order_ref[a_ * inner * cores + j], base)
+        key_pos = base * span + lane % span
+        key_pos = jnp.where(key_pos < limit, key_pos, FAR)
+        allowed = key_pos <= row_pos
+        for g in range(KVH):
+            kk = kbuf[a_, :, g * HD : (g + 1) * HD]
+            vv = vbuf[a_, :, g * HD : (g + 1) * HD]
+            sc = lax.dot_general(
+                queries[g], kk, (((1,), (1,)), ((), ())), preferred_element_type=jnp.float32
+            )
+            sc = jnp.where(allowed, sc, LOW)
+            best = jnp.max(sc, axis=1, keepdims=True)
+            if state[g] is not None:
+                best = jnp.maximum(best, state[g][0])
+            w = jnp.exp2((sc - best) * log2_scale)
+            tot = jnp.sum(w, axis=1, keepdims=True)
+            o = jnp.dot(w.astype(jnp.bfloat16), vv, preferred_element_type=jnp.float32)
+            if state[g] is not None:
+                old, old_tot, old_o = state[g]
+                f = jnp.exp2((old - best) * log2_scale)
+                tot = tot + old_tot * f
+                o = o + old_o * f
+            state[g] = (best, tot, o)
+
+    def decode_combine():
+        for k in range(n_seq - 1):
+            pltpu.make_async_remote_copy(
+                src_ref=part_out.at[0],
+                dst_ref=part_in.at[k],
+                send_sem=part_send.at[0],
+                recv_sem=part_recv.at[k],
+                device_id={"seq": seq},
+                device_id_type=MESH,
+            ).wait_recv()
+        parts = [part_out[seq]] + [part_in[k] for k in range(n_seq - 1)]
+        tops = [p[1][:, 0:1] for p in parts]
+        tots = [p[1][:, HD - 1 : HD] for p in parts]
+        top = functools.reduce(jnp.maximum, tops)
+        fs = [jnp.exp(t - top) for t in tops]
+        tot = sum(f * t for f, t in zip(fs, tots))
+        o = sum(f * p[0] for f, p in zip(fs, parts))
+        done[seq] = (o / tot).astype(jnp.bfloat16)
+        copies = []
+        for d in range(1, n_seq):
+            peer = (seq + d) % n_seq
+            copy = pltpu.make_async_remote_copy(
+                src_ref=done.at[seq],
+                dst_ref=done.at[seq],
+                send_sem=done_send.at[d - 1],
+                recv_sem=done_recv.at[seq],
+                device_id={"seq": peer},
+                device_id_type=MESH,
+            )
+            copy.start()
+            copies.append(copy)
+        return copies
+
+    done_copies = []
+    for k in range(outer):
+        if k + 1 < outer:
+            await_block(planes[k + 1], b, core)
+            to_inner(planes[k + 1], b, core)
+            to_core(planes[k + 1], b, core)
+        for d in range(1, inner):
+            await_block(planes[k], (b + d) % inner, core)
+            to_core(planes[k], (b + d) % inner, core)
+        if k == outer - 1:
+            done_copies = decode_combine()
+        for d in range(1, cores):
+            for d2 in range(inner):
+                await_block(planes[k], (b + d2) % inner, (core + d) % cores)
+        attend(planes[k])
+
+    live = row_pos < limit
+    for g in range(KVH):
+        _, tot, o = state[g]
+        res = jnp.where(live, o / tot, 0.0).astype(jnp.bfloat16)
+        for h in range(group):
+            out_ref[:, (g * group + h) * HD : (g * group + h + 1) * HD] = res[
+                h * span : (h + 1) * span
+            ]
+
+    for d in range(1, n_seq):
+        peer = (seq + d) % n_seq
+        pltpu.make_async_remote_copy(
+            src_ref=done.at[peer],
+            dst_ref=done.at[peer],
+            send_sem=done_send.at[0],
+            recv_sem=done_recv.at[peer],
+            device_id={"seq": seq},
+            device_id_type=MESH,
+        ).wait_recv()
+    flat[...] = done[...].reshape(flat.shape).astype(jnp.float32)
+    for h in range(group):
+        dec_ref[:, h * HD : (h + 1) * HD] = flat[pl.ds(h, sessions, stride=8), :].astype(
+            jnp.bfloat16
+        )
+    for copy in sends + part_copies + done_copies:
+        copy.wait_send()
+
+
+def fused(outer, inner, cores, *args):
+    pq, pk, pv, length, order, nq, nk, nv, ck, cv, clen = args
+    span = pq.shape[0]
+    sessions = nq.shape[0]
+    n_seq = outer * inner
+    per = sessions // n_seq
+    n_sends = (outer - 1) + outer * (inner - 1) + n_seq * (cores - 1)
+    keys = inner * cores * span
+    hbm = pl.BlockSpec(memory_space=pl.ANY)
+    vmem = pl.BlockSpec(memory_space=pltpu.VMEM)
+    smem = pl.BlockSpec(memory_space=pltpu.SMEM)
+    dma = pltpu.SemaphoreType.DMA
+    return pl.pallas_call(
+        functools.partial(fused_kernel, outer, inner, cores),
+        name="attention",
+        out_shape=(
+            jax.ShapeDtypeStruct(pq.shape, jnp.bfloat16),
+            jax.ShapeDtypeStruct(nq.shape, jnp.bfloat16),
+        ),
+        in_specs=[hbm, hbm, hbm, smem, smem, vmem, vmem, vmem, hbm, hbm, smem],
+        out_specs=(vmem, vmem),
+        scratch_shapes=[
+            pltpu.VMEM(pq.shape, jnp.bfloat16),
+            pltpu.VMEM((outer, keys, pk.shape[1]), jnp.bfloat16),
+            pltpu.VMEM((outer, keys, pv.shape[1]), jnp.bfloat16),
+            pltpu.VMEM(ck.shape, jnp.bfloat16),
+            pltpu.VMEM(cv.shape, jnp.bfloat16),
+            pltpu.VMEM((8 * sessions, HD), jnp.float32),
+            pltpu.VMEM((n_seq, 2, per * 8, HD), jnp.float32),
+            pltpu.VMEM((n_seq - 1, 2, per * 8, HD), jnp.float32),
+            pltpu.VMEM((n_seq, per * 8, HD), jnp.bfloat16),
+            pltpu.VMEM((8 * sessions, HD), jnp.float32),
+            dma((5,)),
+            dma((2, n_sends)),
+            dma((2, n_seq * cores)),
+            dma((n_seq - 1,)),
+            dma((n_seq - 1,)),
+            dma((n_seq - 1,)),
+            dma((n_seq,)),
+        ],
+        compiler_params=pltpu.CompilerParams(
+            collective_id=0, has_side_effects=True, vmem_limit_bytes=48 * 1024 * 1024
+        ),
+    )(*args)
+
+
+def per_device(outer, inner, cores, *args):
+    sessions, span = args[5].shape[0], args[0].shape[0]
+    if sessions % (outer * inner) or span % 16 or QH // KVH > 8:
+        return composed(*args)
+    return fused(outer, inner, cores, *args)
+
+
 def solution(mesh):
+    n_seq, cores = mesh.shape["seq"], mesh.shape["head"]
+    inner = max(d for d in range(1, math.isqrt(n_seq) + 1) if n_seq % d == 0)
     return jax.shard_map(
-        per_device,
+        functools.partial(per_device, n_seq // inner, inner, cores),
         mesh=mesh,
         in_specs=(
             P(("rep", "seq", "head"), None),

time: 116 us -> 35.4 us (0.31)
  blocking collectives: 98.5 us -> 0 us
  Pallas kernels: 0 us -> 25.3 us
  other arithmetic: 5.16 us -> 0 us
  loops' own time: 2.84 us -> 0 us
  local copies, waits for them, and re-layouts: 5.63 us -> 8.32 us
  matrix products: 2.11 us -> 0 us
    all_gather x2 -> x0, blocking collectives: 43.7 us -> none  [the longest x1 24.8 us: per_device(): lax.all_gather(prompt_key, ('seq', 'head'), axis=0, tiled=True)]
    psum x1 -> x0, blocking collectives: 33.8 us -> none  [per_device(): lax.psum((row_total * factor, weighted * factor[..., None]), 'seq')]
    pallas_call x0 -> x1, Pallas kernels: none -> 25.3 us  [fused(): pl.pallas_call(functools.partial(fused_kernel, outer, inner, cores), name...]
    pmax x1 -> x0, blocking collectives: 21 us -> none  [per_device(): global_max = lax.pmax(row_max, 'seq')]
    unnamed x17 -> x22, local copies, waits for them, and re-layouts: 0.67 us -> 8.32 us
    another operation x3 -> x0, loops' own time: 2.84 us -> none  [the longest x1 2.77 us: attend_rows(): lax.scan(advance, running, jnp.arange(key_count // block_rows, dtype=jnp....]
    dot_general x5 -> x0, matrix products: 2.11 us -> none  [the longest x1 0.74 us: compute(): jnp.einsum('kgrn,nkd->kgrd', weights.astype(jnp.bfloat16), value_block, p...]
    reduce_sum x5 -> x0, other arithmetic: 1.72 us -> none  [the longest x3 0.92 us: lookup(): picked = jnp.sum(jnp.where(chosen, span_table[None, :], 0), axis=1)]
where the time goes in v1:
time: 35.4 us; the launch traced here: 34.9 us
  Pallas kernels  25.3 us (71%)
  local copies, waits for them, and re-layouts  8.32 us (24%)
  between operations  1.35 us (4%)
    pallas_call x1, Pallas kernels, fused(): pl.pallas_call(functools.partial(fused_kernel, outer, inner, cores), name...  25.3 us
    unnamed x22, local copies, waits for them, and re-layouts  8.32 us

profile of v1, /device:TPU:0, one launch (start us, length us, event | category | flops | bytes accessed | tf_op | source)
XLA Modules:
  0.0 34.9 jit_solution(12899874680073913824)
XLA Ops:
  0.6 0.0 copy-start.9
  0.6 0.0 copy-start.8
  1.3 0.0 copy-done.9
  1.3 0.0 copy-done.8
  1.3 0.0 copy-start
  1.3 1.2 %copy-done = bf16[16,1,256,128]{3,2,1,0:T(8,128)(2,1)S(1)} copy-done((bf16[16,1,256,128]{3,2,1,0:T(8,128)(2,1)S(1)}, bf16[16,1,256,128]{3,2,1,0:T(8,128)(2,1)}, u32[]{:S(2)}) %copy-start) | copy-done | bytes 1048600
  2.6 0.0 copy-start.1
  2.6 1.2 %copy-done.1 = bf16[16,1,256,128]{3,2,1,0:T(8,128)(2,1)S(1)} copy-done((bf16[16,1,256,128]{3,2,1,0:T(8,128)(2,1)S(1)}, bf16[16,1,256,128]{3,2,1,0:T(8,128)(2,1)}, u32[]{:S(2)}) %copy-start.1) | copy-done | bytes 1048600
  3.8 0.0 copy-start.2
  3.8 0.9 %copy-done.2 = bf16[64,1792]{1,0:T(8,128)(2,1)S(1)} copy-done((bf16[64,1792]{1,0:T(8,128)(2,1)S(1)}, bf16[64,1792]{1,0:T(8,128)(2,1)}, u32[]{:S(2)}) %copy-start.2) | copy-done | bytes 229400
  4.7 0.0 copy-start.3
  4.7 0.8 %copy-done.3 = bf16[64,256]{1,0:T(8,128)(2,1)S(1)} copy-done((bf16[64,256]{1,0:T(8,128)(2,1)S(1)}, bf16[64,256]{1,0:T(8,128)(2,1)}, u32[]{:S(2)}) %copy-start.3) | copy-done | bytes 32792
  5.5 0.0 copy-start.4
  5.5 0.8 %copy-done.4 = bf16[64,256]{1,0:T(8,128)(2,1)S(1)} copy-done((bf16[64,256]{1,0:T(8,128)(2,1)S(1)}, bf16[64,256]{1,0:T(8,128)(2,1)}, u32[]{:S(2)}) %copy-start.4) | copy-done | bytes 32792
  6.2 0.0 copy-start.5
  6.2 0.7 %copy-done.5 = bf16[16,896]{1,0:T(8,128)(2,1)S(1)} copy-done((bf16[16,896]{1,0:T(8,128)(2,1)S(1)}, bf16[16,896]{1,0:T(8,128)(2,1)}, u32[]{:S(2)}) %copy-start.5) | copy-done | bytes 28696
  7.0 0.0 copy-start.6
  7.0 0.7 %copy-done.6 = bf16[16,128]{1,0:T(8,128)(2,1)S(1)} copy-done((bf16[16,128]{1,0:T(8,128)(2,1)S(1)}, bf16[16,128]{1,0:T(8,128)(2,1)}, u32[]{:S(2)}) %copy-start.6) | copy-done | bytes 4120
  7.7 0.0 copy-start.7
  7.7 0.7 %copy-done.7 = bf16[16,128]{1,0:T(8,128)(2,1)S(1)} copy-done((bf16[16,128]{1,0:T(8,128)(2,1)S(1)}, bf16[16,128]{1,0:T(8,128)(2,1)}, u32[]{:S(2)}) %copy-start.7) | copy-done | bytes 4120
  8.4 25.3 %attention.1 = (bf16[64,1792]{1,0:T(8,128)(2,1)S(1)}, bf16[16,896]{1,0:T(8,128)(2,1)S(1)}) custom-call(bf16[64,1792]{1,0:T(8,128)(2,1)S(1)} %copy-done.2, bf16[64,256]{1,0:T(8,128)(2,1)S(1)} %copy-done.3, bf16[64,256]{1,0:T(8,128)(2,1)S(1)} %copy-done.4, s32[1]{0:T(128)S(6)} %copy.15.length_ref, s32[16]{0:T(128)S(1)} %copy-done.8, ...), custom_call_target="tpu_custom_call" | custom-call | tf_op jit(solution)/shard_map/attention/pallas_call | solution.py:455
  33.6 0.7 %copy.16 = bf16[64,1792]{1,0:T(8,128)(2,1)} copy(bf16[64,1792]{1,0:T(8,128)(2,1)S(1)} %get-tuple-element.4) | data formatting | bytes 458752
  34.3 0.6 %copy.17 = bf16[16,896]{1,0:T(8,128)(2,1)} copy(bf16[16,896]{1,0:T(8,128)(2,1)S(1)} %get-tuple-element.5) | data formatting | bytes 57344
Async XLA Ops:
  0.6 0.7 %copy-start.9 = (s32[16]{0:T(128)S(1)}, s32[16]{0:T(128)}, u32[]{:S(2)}) copy-start(s32[16]{0:T(128)} %clen_ref.1) | copy-start | bytes 196
  0.6 0.7 %copy-start.8 = (s32[16]{0:T(128)S(1)}, s32[16]{0:T(128)}, u32[]{:S(2)}) copy-start(s32[16]{0:T(128)} %order_ref.1) | copy-start | bytes 196
  1.3 1.2 %copy-start = (bf16[16,1,256,128]{3,2,1,0:T(8,128)(2,1)S(1)}, bf16[16,1,256,128]{3,2,1,0:T(8,128)(2,1)}, u32[]{:S(2)}) copy-start(bf16[16,1,256,128]{3,2,1,0:T(8,128)(2,1)} %ck_hbm.1) | copy-start | bytes 3145732
  2.6 1.2 %copy-start.1 = (bf16[16,1,256,128]{3,2,1,0:T(8,128)(2,1)S(1)}, bf16[16,1,256,128]{3,2,1,0:T(8,128)(2,1)}, u32[]{:S(2)}) copy-start(bf16[16,1,256,128]{3,2,1,0:T(8,128)(2,1)} %cv_hbm.1) | copy-start | bytes 3145732
  3.8 0.9 %copy-start.2 = (bf16[64,1792]{1,0:T(8,128)(2,1)S(1)}, bf16[64,1792]{1,0:T(8,128)(2,1)}, u32[]{:S(2)}) copy-start(bf16[64,1792]{1,0:T(8,128)(2,1)} %pq_hbm.1) | copy-start | bytes 688132
  4.7 0.8 %copy-start.3 = (bf16[64,256]{1,0:T(8,128)(2,1)S(1)}, bf16[64,256]{1,0:T(8,128)(2,1)}, u32[]{:S(2)}) copy-start(bf16[64,256]{1,0:T(8,128)(2,1)} %pk_hbm.1) | copy-start | bytes 98308
  5.5 0.8 %copy-start.4 = (bf16[64,256]{1,0:T(8,128)(2,1)S(1)}, bf16[64,256]{1,0:T(8,128)(2,1)}, u32[]{:S(2)}) copy-start(bf16[64,256]{1,0:T(8,128)(2,1)} %pv_hbm.1) | copy-start | bytes 98308
  6.2 0.7 %copy-start.5 = (bf16[16,896]{1,0:T(8,128)(2,1)S(1)}, bf16[16,896]{1,0:T(8,128)(2,1)}, u32[]{:S(2)}) copy-start(bf16[16,896]{1,0:T(8,128)(2,1)} %nq_ref.1) | copy-start | bytes 86020
  7.0 0.7 %copy-start.6 = (bf16[16,128]{1,0:T(8,128)(2,1)S(1)}, bf16[16,128]{1,0:T(8,128)(2,1)}, u32[]{:S(2)}) copy-start(bf16[16,128]{1,0:T(8,128)(2,1)} %nk_ref.1) | copy-start | bytes 12292
  7.7 0.7 %copy-start.7 = (bf16[16,128]{1,0:T(8,128)(2,1)S(1)}, bf16[16,128]{1,0:T(8,128)(2,1)}, u32[]{:S(2)}) copy-start(bf16[16,128]{1,0:T(8,128)(2,1)} %nv_ref.1) | copy-start | bytes 12292

commit v2 on v1

--- a/solution.py
+++ b/solution.py
@@ -181,9 +181,10 @@
 
 def fused_kernel(
     outer, inner, cores,
-    pq_hbm, pk_hbm, pv_hbm, length_ref, order_ref, nq_ref, nk_ref, nv_ref, ck_hbm, cv_hbm, clen_ref,
+    pq_hbm, pk_hbm, pv_hbm, length_ref, order_ref, nq_hbm, nk_hbm, nv_hbm, ck_hbm, cv_hbm, clen_ref,
     out_ref, dec_ref,
-    pq, kbuf, vbuf, ck, cv, qrows, part_out, part_in, done, flat,
+    pq, kbuf, vbuf, ck, cv, nq_ref, nk_ref, nv_ref, qrows, sum_out, sum_in, stat_out, stat_in,
+    done, flat,
     in_sem, kv_send, kv_recv, part_send, part_recv, done_send, done_recv,
 ):
     group = QH // KVH
@@ -207,6 +208,9 @@
         pltpu.make_async_copy(ck_hbm, ck, in_sem.at[2]),
         pltpu.make_async_copy(cv_hbm, cv, in_sem.at[3]),
         pltpu.make_async_copy(pq_hbm, pq, in_sem.at[4]),
+        pltpu.make_async_copy(nq_hbm, nq_ref, in_sem.at[5]),
+        pltpu.make_async_copy(nk_hbm, nk_ref, in_sem.at[6]),
+        pltpu.make_async_copy(nv_hbm, nv_ref, in_sem.at[7]),
     ]
     for copy in local:
         copy.start()
@@ -226,52 +230,58 @@
 
     sends = []
 
-    def send(a_, b_, c_, target):
-        block = block_id(a_, b_, c_)
-        for which, buf in ((0, kbuf), (1, vbuf)):
-            ref = buf.at[a_, rows_of(b_, c_)]
-            copy = pltpu.make_async_remote_copy(
-                src_ref=ref,
-                dst_ref=ref,
-                send_sem=kv_send.at[which, len(sends) // 2],
-                recv_sem=kv_recv.at[which, block],
-                device_id=target,
-                device_id_type=MESH,
-            )
-            copy.start()
-            sends.append(copy)
-
-    def await_block(a_, b_, c_):
-        block = block_id(a_, b_, c_)
-        for which, buf in ((0, kbuf), (1, vbuf)):
-            ref = buf.at[a_, rows_of(b_, c_)]
-            pltpu.make_async_remote_copy(
-                src_ref=ref,
-                dst_ref=ref,
-                send_sem=kv_send.at[which, 0],
-                recv_sem=kv_recv.at[which, block],
-                device_id={"seq": seq},
-                device_id_type=MESH,
-            ).wait_recv()
-
-    def to_inner(a_, b_, c_):
+    bufs = (kbuf, vbuf)
+
+    def send(which, a_, b_, c_, target):
+        ref = bufs[which].at[a_, rows_of(b_, c_)]
+        copy = pltpu.make_async_remote_copy(
+            src_ref=ref,
+            dst_ref=ref,
+            send_sem=kv_send.at[len(sends)],
+            recv_sem=kv_recv.at[which, block_id(a_, b_, c_)],
+            device_id=target,
+            device_id_type=MESH,
+        )
+        copy.start()
+        sends.append(copy)
+
+    def await_block(which, a_, b_, c_):
+        ref = bufs[which].at[a_, rows_of(b_, c_)]
+        pltpu.make_async_remote_copy(
+            src_ref=ref,
+            dst_ref=ref,
+            send_sem=kv_send.at[0],
+            recv_sem=kv_recv.at[which, block_id(a_, b_, c_)],
+            device_id={"seq": seq},
+            device_id_type=MESH,
+        ).wait_recv()
+
+    def to_inner(which, a_, b_, c_):
         for d in range(1, inner):
-            send(a_, b_, c_, {"seq": a * inner + (b + d) % inner})
-
-    def to_core(a_, b_, c_):
+            send(which, a_, b_, c_, {"seq": a * inner + (b + d) % inner})
+
+    def to_core(which, a_, b_, c_):
         for d in range(1, cores):
-            send(a_, b_, c_, {"head": (core + d) % cores})
+            send(which, a_, b_, c_, {"head": (core + d) % cores})
 
     nearest = [sorted(range(outer), key=lambda p, i=i: (abs(p - i), p)) for i in range(outer)]
     planes = [pick(a, [nearest[i][k] for i in range(outer)]) for k in range(outer)]
 
-    to_inner(a, b, core)
-    for k in range(1, outer):
-        send(a, b, core, {"seq": planes[k] * inner + b})
-    to_core(a, b, core)
+    for which in range(2):
+        to_inner(which, a, b, core)
+        if outer > 1:
+            send(which, a, b, core, {"seq": planes[1] * inner + b})
+    for k in range(2, outer):
+        for which in range(2):
+            send(which, a, b, core, {"seq": planes[k] * inner + b})
+    for which in range(2):
+        to_core(which, a, b, core)
 
     sessions, ctx = ck.shape[0], ck.shape[2]
     per = sessions // n_seq
+    field = HD // (2 * per)
+    for copy in local[5:]:
+        copy.wait()
     for h in range(8):
         if h < group:
             qrows[pl.ds(h * sessions, sessions), :] = nq_ref[:, h * HD : (h + 1) * HD].astype(
@@ -303,23 +313,30 @@
         o = jnp.dot(w.astype(jnp.bfloat16), cv[s, 0], preferred_element_type=jnp.float32)
         o = o + own_w.astype(jnp.bfloat16).astype(jnp.float32) * nv[s : s + 1, :]
         lane = lax.broadcasted_iota(jnp.int32, (8, HD), 1)
-        dst, row = s // per, (s % per) * 8
-        part_out[dst, 0, pl.ds(row, 8), :] = o
-        part_out[dst, 1, pl.ds(row, 8), :] = jnp.where(lane < HD // 2, top, tot)
+        dst, at = s // per, s % per
+        if at == 0:
+            outs, stats = [], jnp.zeros((8, HD), jnp.float32)
+        outs.append(o)
+        stats = jnp.where(lane // field == 2 * at, top, stats)
+        stats = jnp.where(lane // field == 2 * at + 1, tot, stats)
+        if at == per - 1:
+            sum_out[dst] = jnp.concatenate(outs, axis=0).astype(jnp.bfloat16)
+            stat_out[dst] = stats
 
     part_copies = []
     for d in range(1, n_seq):
         peer = (seq + d) % n_seq
-        copy = pltpu.make_async_remote_copy(
-            src_ref=part_out.at[peer],
-            dst_ref=part_in.at[n_seq - 1 - d],
-            send_sem=part_send.at[d - 1],
-            recv_sem=part_recv.at[n_seq - 1 - d],
-            device_id={"seq": peer},
-            device_id_type=MESH,
-        )
-        copy.start()
-        part_copies.append(copy)
+        for which, out, into in ((0, stat_out, stat_in), (1, sum_out, sum_in)):
+            copy = pltpu.make_async_remote_copy(
+                src_ref=out.at[peer],
+                dst_ref=into.at[n_seq - 1 - d],
+                send_sem=part_send.at[which, d - 1],
+                recv_sem=part_recv.at[which, n_seq - 1 - d],
+                device_id={"seq": peer},
+                device_id_type=MESH,
+            )
+            copy.start()
+            part_copies.append(copy)
 
     local[4].wait()
     me_block = block_id(a, b, core)
@@ -365,21 +382,35 @@
 
     def decode_combine():
         for k in range(n_seq - 1):
-            pltpu.make_async_remote_copy(
-                src_ref=part_out.at[0],
-                dst_ref=part_in.at[k],
-                send_sem=part_send.at[0],
-                recv_sem=part_recv.at[k],
-                device_id={"seq": seq},
-                device_id_type=MESH,
-            ).wait_recv()
-        parts = [part_out[seq]] + [part_in[k] for k in range(n_seq - 1)]
-        tops = [p[1][:, 0:1] for p in parts]
-        tots = [p[1][:, HD - 1 : HD] for p in parts]
+            for which, out, into in ((0, stat_out, stat_in), (1, sum_out, sum_in)):
+                pltpu.make_async_remote_copy(
+                    src_ref=out.at[0],
+                    dst_ref=into.at[k],
+                    send_sem=part_send.at[which, 0],
+                    recv_sem=part_recv.at[which, k],
+                    device_id={"seq": seq},
+                    device_id_type=MESH,
+                ).wait_recv()
+        stats = [stat_out[seq]] + [stat_in[k] for k in range(n_seq - 1)]
+        sums = [sum_out[seq]] + [sum_in[k] for k in range(n_seq - 1)]
+
+        def spread(which):
+            return [
+                jnp.concatenate(
+                    [
+                        x[:, (2 * at + which) * field : (2 * at + which) * field + 1]
+                        for at in range(per)
+                    ],
+                    axis=0,
+                )
+                for x in stats
+            ]
+
+        tops, tots = spread(0), spread(1)
         top = functools.reduce(jnp.maximum, tops)
         fs = [jnp.exp(t - top) for t in tops]
         tot = sum(f * t for f, t in zip(fs, tots))
-        o = sum(f * p[0] for f, p in zip(fs, parts))
+        o = sum(f * x.astype(jnp.float32) for f, x in zip(fs, sums))
         done[seq] = (o / tot).astype(jnp.bfloat16)
         copies = []
         for d in range(1, n_seq):
@@ -399,17 +430,20 @@
     done_copies = []
     for k in range(outer):
         if k + 1 < outer:
-            await_block(planes[k + 1], b, core)
-            to_inner(planes[k + 1], b, core)
-            to_core(planes[k + 1], b, core)
-        for d in range(1, inner):
-            await_block(planes[k], (b + d) % inner, core)
-            to_core(planes[k], (b + d) % inner, core)
-        if k == outer - 1:
+            for which in range(2):
+                await_block(which, planes[k + 1], b, core)
+                to_inner(which, planes[k + 1], b, core)
+                to_core(which, planes[k + 1], b, core)
+        for which in range(2):
+            for d in range(1, inner):
+                await_block(which, planes[k], (b + d) % inner, core)
+                to_core(which, planes[k], (b + d) % inner, core)
+        if k == max(outer - 2, 0):
             done_copies = decode_combine()
         for d in range(1, cores):
             for d2 in range(inner):
-                await_block(planes[k], (b + d2) % inner, (core + d) % cores)
+                for which in range(2):
+                    await_block(which, planes[k], (b + d2) % inner, (core + d) % cores)
         attend(planes[k])
 
     live = row_pos < limit
@@ -440,6 +474,17 @@
         copy.wait_send()
 
 
+def store_kernel(prompt_ref, decode_ref, prompt_out, decode_out, sem):
+    copies = [
+        pltpu.make_async_copy(prompt_ref, prompt_out, sem.at[0]),
+        pltpu.make_async_copy(decode_ref, decode_out, sem.at[1]),
+    ]
+    for copy in copies:
+        copy.start()
+    for copy in copies:
+        copy.wait()
+
+
 def fused(outer, inner, cores, *args):
     pq, pk, pv, length, order, nq, nk, nv, ck, cv, clen = args
     span = pq.shape[0]
@@ -448,18 +493,18 @@
     per = sessions // n_seq
     n_sends = (outer - 1) + outer * (inner - 1) + n_seq * (cores - 1)
     keys = inner * cores * span
-    hbm = pl.BlockSpec(memory_space=pl.ANY)
+    hbm = pl.BlockSpec(memory_space=pltpu.HBM)
     vmem = pl.BlockSpec(memory_space=pltpu.VMEM)
     smem = pl.BlockSpec(memory_space=pltpu.SMEM)
     dma = pltpu.SemaphoreType.DMA
-    return pl.pallas_call(
+    results = pl.pallas_call(
         functools.partial(fused_kernel, outer, inner, cores),
         name="attention",
         out_shape=(
             jax.ShapeDtypeStruct(pq.shape, jnp.bfloat16),
             jax.ShapeDtypeStruct(nq.shape, jnp.bfloat16),
         ),
-        in_specs=[hbm, hbm, hbm, smem, smem, vmem, vmem, vmem, hbm, hbm, smem],
+        in_specs=[hbm, hbm, hbm, smem, smem, hbm, hbm, hbm, hbm, hbm, smem],
         out_specs=(vmem, vmem),
         scratch_shapes=[
             pltpu.VMEM(pq.shape, jnp.bfloat16),
@@ -467,23 +512,42 @@
             pltpu.VMEM((outer, keys, pv.shape[1]), jnp.bfloat16),
             pltpu.VMEM(ck.shape, jnp.bfloat16),
             pltpu.VMEM(cv.shape, jnp.bfloat16),
+            pltpu.VMEM(nq.shape, jnp.bfloat16),
+            pltpu.VMEM(nk.shape, jnp.bfloat16),
+            pltpu.VMEM(nv.shape, jnp.bfloat16),
             pltpu.VMEM((8 * sessions, HD), jnp.float32),
-            pltpu.VMEM((n_seq, 2, per * 8, HD), jnp.float32),
-            pltpu.VMEM((n_seq - 1, 2, per * 8, HD), jnp.float32),
+            pltpu.VMEM((n_seq, per * 8, HD), jnp.bfloat16),
+            pltpu.VMEM((n_seq - 1, per * 8, HD), jnp.bfloat16),
+            pltpu.VMEM((n_seq, 8, HD), jnp.float32),
+            pltpu.VMEM((n_seq - 1, 8, HD), jnp.float32),
             pltpu.VMEM((n_seq, per * 8, HD), jnp.bfloat16),
             pltpu.VMEM((8 * sessions, HD), jnp.float32),
-            dma((5,)),
-            dma((2, n_sends)),
+            dma((8,)),
+            dma((2 * n_sends,)),
             dma((2, n_seq * cores)),
-            dma((n_seq - 1,)),
-            dma((n_seq - 1,)),
+            dma((2, n_seq - 1)),
+            dma((2, n_seq - 1)),
             dma((n_seq - 1,)),
             dma((n_seq,)),
         ],
         compiler_params=pltpu.CompilerParams(
             collective_id=0, has_side_effects=True, vmem_limit_bytes=48 * 1024 * 1024
         ),
-    )(*args)
+    )(
+        *(
+            x if x.dtype == jnp.int32 else pltpu.with_memory_space_constraint(x, pltpu.HBM)
+            for x in args
+        )
+    )
+    return pl.pallas_call(
+        store_kernel,
+        name="store",
+        out_shape=tuple(jax.ShapeDtypeStruct(x.shape, x.dtype) for x in results),
+        in_specs=[pl.BlockSpec(memory_space=pl.ANY)] * 2,
+        out_specs=(pl.BlockSpec(memory_space=pl.ANY),) * 2,
+        scratch_shapes=[dma((2,))],
+        compiler_params=pltpu.CompilerParams(vmem_limit_bytes=4 * 1024 * 1024),
+    )(*results)
 
 
 def per_device(outer, inner, cores, *args):

time: 35.4 us -> 25.1 us (0.71)
  local copies, waits for them, and re-layouts: 8.32 us -> 0.01 us
  Pallas kernels: 25.3 us -> 23.6 us
    unnamed x22 -> x4, local copies, waits for them, and re-layouts: 8.32 us -> 0.01 us
    pallas_call x1, Pallas kernels: 25.3 us -> 22.9 us  [fused(): pl.pallas_call(functools.partial(fused_kernel, outer, inner, cores), name...]
    pallas_call x0 -> x1, Pallas kernels: none -> 0.71 us  [fused(): pl.pallas_call(store_kernel, name='store', out_shape=tuple((jax.ShapeDtyp...]
where the time goes in v2:
time: 25.1 us; the launch traced here: 25 us
  Pallas kernels  23.6 us (94%)
  between operations  1.34 us (5%)
    pallas_call x1, Pallas kernels, fused(): pl.pallas_call(functools.partial(fused_kernel, outer, inner, cores), name...  22.9 us
    pallas_call x1, Pallas kernels, fused(): pl.pallas_call(store_kernel, name='store', out_shape=tuple((jax.ShapeDtyp...  0.71 us

profile of v2, /device:TPU:0, one launch (start us, length us, event | category | flops | bytes accessed | tf_op | source)
XLA Modules:
  0.0 25.0 jit_solution(11368339627712552612)
XLA Ops:
  0.6 0.0 copy-start.1
  0.6 0.0 copy-start
  1.3 0.0 copy-done.1
  1.3 0.0 copy-done
  1.3 22.9 %attention.1 = (bf16[64,1792]{1,0:T(8,128)(2,1)S(1)}, bf16[16,896]{1,0:T(8,128)(2,1)S(1)}) custom-call(bf16[64,1792]{1,0:T(8,128)(2,1)} %pq_hbm.1, bf16[64,256]{1,0:T(8,128)(2,1)} %pk_hbm.1, bf16[64,256]{1,0:T(8,128)(2,1)} %pv_hbm.1, s32[1]{0:T(128)S(6)} %copy.13.length_ref, s32[16]{0:T(128)S(1)} %copy-done, bf16[16,896]{1,0:T(8,128)(2,1)} %nq_hbm.1, ...), custom_call_target="tpu_custom_call" | custom-call | tf_op jit(solution)/shard_map/attention/pallas_call | solution.py:500
  24.3 0.7 %store.1 = (bf16[64,1792]{1,0:T(8,128)(2,1)}, bf16[16,896]{1,0:T(8,128)(2,1)}) custom-call(bf16[64,1792]{1,0:T(8,128)(2,1)S(1)} %get-tuple-element.4.prompt_ref, bf16[16,896]{1,0:T(8,128)(2,1)S(1)} %get-tuple-element.5.decode_ref), custom_call_target="tpu_custom_call" | custom-call | tf_op jit(solution)/shard_map/store/pallas_call | solution.py:542
Async XLA Ops:
  0.6 0.7 %copy-start.1 = (s32[16]{0:T(128)S(1)}, s32[16]{0:T(128)}, u32[]{:S(2)}) copy-start(s32[16]{0:T(128)} %clen_ref.1) | copy-start | bytes 196
  0.6 0.7 %copy-start = (s32[16]{0:T(128)S(1)}, s32[16]{0:T(128)}, u32[]{:S(2)}) copy-start(s32[16]{0:T(128)} %order_ref.1) | copy-start | bytes 196

commit v3 on v2

--- a/solution.py
+++ b/solution.py
@@ -185,7 +185,7 @@
     out_ref, dec_ref,
     pq, kbuf, vbuf, ck, cv, nq_ref, nk_ref, nv_ref, qrows, sum_out, sum_in, stat_out, stat_in,
     done, flat,
-    in_sem, kv_send, kv_recv, part_send, part_recv, done_send, done_recv,
+    in_sem, kv_send, kv_recv, part_send, part_recv, done_send, done_recv, hello,
 ):
     group = QH // KVH
     span = kbuf.shape[1] // (inner * cores)
@@ -216,17 +216,35 @@
         copy.start()
 
     barrier = pltpu.get_barrier_semaphore()
-    for d in range(1, n_seq):
-        pl.semaphore_signal(
-            barrier, inc=1, device_id={"seq": (seq + d) % n_seq}, device_id_type=MESH
-        )
+
+    def greet_line(sem):
+        for step, there in ((-1, a > 0), (1, a < outer - 1)):
+
+            @pl.when(there)
+            def _(step=step):
+                pl.semaphore_signal(
+                    sem, inc=1, device_id={"seq": seq + step * inner}, device_id_type=MESH
+                )
+
+    def greet_inner(sem):
+        for d in range(1, inner):
+            pl.semaphore_signal(
+                sem,
+                inc=1,
+                device_id={"seq": a * inner + (b + d) % inner},
+                device_id_type=MESH,
+            )
+
+    beside = jnp.where(a > 0, 1, 0) + jnp.where(a < outer - 1, 1, 0)
+    greet_line(barrier)
+    greet_inner(barrier)
     for d in range(1, cores):
         pl.semaphore_signal(
             barrier, inc=1, device_id={"head": (core + d) % cores}, device_id_type=MESH
         )
     local[0].wait()
     local[1].wait()
-    pl.semaphore_wait(barrier, n_seq - 1 + cores - 1)
+    pl.semaphore_wait(barrier, beside + inner - 1 + cores - 1)
 
     sends = []
 
@@ -264,13 +282,17 @@
         for d in range(1, cores):
             send(which, a_, b_, c_, {"head": (core + d) % cores})
 
-    nearest = [sorted(range(outer), key=lambda p, i=i: (abs(p - i), p)) for i in range(outer)]
+    nearest = [sorted(range(outer), key=lambda p, i=i: (abs(p - i), abs(2 * p - outer + 1))) for i in range(outer)]
     planes = [pick(a, [nearest[i][k] for i in range(outer)]) for k in range(outer)]
 
     for which in range(2):
         to_inner(which, a, b, core)
         if outer > 1:
             send(which, a, b, core, {"seq": planes[1] * inner + b})
+    for r in range(outer - 2):
+        greet_line(hello.at[r])
+        pl.semaphore_wait(hello.at[r], beside)
+    greet_inner(hello.at[outer - 1])
     for k in range(2, outer):
         for which in range(2):
             send(which, a, b, core, {"seq": planes[k] * inner + b})
@@ -323,6 +345,7 @@
             sum_out[dst] = jnp.concatenate(outs, axis=0).astype(jnp.bfloat16)
             stat_out[dst] = stats
 
+    pl.semaphore_wait(hello.at[outer - 1], inner - 1)
     part_copies = []
     for d in range(1, n_seq):
         peer = (seq + d) % n_seq
@@ -529,6 +552,7 @@
             dma((2, n_seq - 1)),
             dma((n_seq - 1,)),
             dma((n_seq,)),
+            pltpu.SemaphoreType.REGULAR((outer,)),
         ],
         compiler_params=pltpu.CompilerParams(
             collective_id=0, has_side_effects=True, vmem_limit_bytes=48 * 1024 * 1024

time: 25.1 us -> 24.1 us (0.960)
  Pallas kernels: 23.6 us -> 22.6 us
    pallas_call x1, Pallas kernels: 22.9 us -> 21.9 us  [fused(): pl.pallas_call(functools.partial(fused_kernel, outer, inner, cores), name...]
where the time goes in v3:
time: 24.1 us; the launch traced here: 24 us
  Pallas kernels  22.6 us (94%)
  between operations  1.34 us (6%)
    pallas_call x1, Pallas kernels, fused(): pl.pallas_call(functools.partial(fused_kernel, outer, inner, cores), name...  21.9 us
    pallas_call x1, Pallas kernels, fused(): pl.pallas_call(store_kernel, name='store', out_shape=tuple((jax.ShapeDtyp...  0.71 us

profile of v3, /device:TPU:0, one launch (start us, length us, event | category | flops | bytes accessed | tf_op | source)
XLA Modules:
  0.0 24.0 jit_solution(2064603124717583174)
XLA Ops:
  0.6 0.0 copy-start.1
  0.6 0.0 copy-start
  1.3 0.0 copy-done.1
  1.3 0.0 copy-done
  1.3 21.9 %attention.1 = (bf16[64,1792]{1,0:T(8,128)(2,1)S(1)}, bf16[16,896]{1,0:T(8,128)(2,1)S(1)}) custom-call(bf16[64,1792]{1,0:T(8,128)(2,1)} %pq_hbm.1, bf16[64,256]{1,0:T(8,128)(2,1)} %pk_hbm.1, bf16[64,256]{1,0:T(8,128)(2,1)} %pv_hbm.1, s32[1]{0:T(128)S(6)} %copy.13.length_ref, s32[16]{0:T(128)S(1)} %copy-done, bf16[16,896]{1,0:T(8,128)(2,1)} %nq_hbm.1, ...), custom_call_target="tpu_custom_call" | custom-call | tf_op jit(solution)/shard_map/attention/pallas_call | solution.py:523
  23.3 0.7 %store.1 = (bf16[64,1792]{1,0:T(8,128)(2,1)}, bf16[16,896]{1,0:T(8,128)(2,1)}) custom-call(bf16[64,1792]{1,0:T(8,128)(2,1)S(1)} %get-tuple-element.4.prompt_ref, bf16[16,896]{1,0:T(8,128)(2,1)S(1)} %get-tuple-element.5.decode_ref), custom_call_target="tpu_custom_call" | custom-call | tf_op jit(solution)/shard_map/store/pallas_call | solution.py:566
Async XLA Ops:
  0.6 0.7 %copy-start.1 = (s32[16]{0:T(128)S(1)}, s32[16]{0:T(128)}, u32[]{:S(2)}) copy-start(s32[16]{0:T(128)} %clen_ref.1) | copy-start | bytes 196
  0.6 0.7 %copy-start = (s32[16]{0:T(128)S(1)}, s32[16]{0:T(128)}, u32[]{:S(2)}) copy-start(s32[16]{0:T(128)} %order_ref.1) | copy-start | bytes 196
